TPU v7x, 32 devices: a whole 2x2x4 slice. The times are simulated.
32 devices in a mesh: dp: 4 (over x, core), tensor: 8 (over z, y).
Axes of the slice: x: 2, y: 2, z: 4, core: 2. Of those that a mesh axis runs over, the one named last changes fastest.
Arguments:
- head_outputs: bfloat16 [4096, 4096], P('dp', 'tensor'), may hold values from -6 to 6
- out_weight: bfloat16 [4096, 4096], P('tensor'), may hold values from -0.09375 to 0.09375
- residual: bfloat16 [4096, 4096], P(('dp', 'tensor')), may hold values from -6 to 6
- norm_gain: float32 [4096], replicated, may hold values from 0.25 to 1.75
- chosen: int32 [16, 256], replicated, may hold values from 0 to 4095, as said below
- gates: float32 [16, 256], replicated, may hold values from 0.25 to 1
- place: int32 [16], replicated, may hold values from 0 to 15, each once
- w_gate: bfloat16 [32, 704, 4096], P(('dp', 'tensor')), may hold values from -0.09375 to 0.09375
- w_up: bfloat16 [32, 704, 4096], P(('dp', 'tensor')), may hold values from -0.09375 to 0.09375
- w_down: bfloat16 [32, 704, 4096], P(('dp', 'tensor')), may hold values from -0.15625 to 0.15625
Outputs:
- mixed: bfloat16 [4096, 4096], P(('dp', 'tensor'))
Inputs may be any that keep to these rules, and one draw needn't show every extreme that they name: `chosen`: row e lists 256 different tokens; at most 16 of them lie in one aligned block of 128 rows (the rows of one device), and in every row some block holds exactly 16.
All inputs are finite; a program needn't handle non-finite values.
Results may differ from a plain program's by a relative error of at most 0.012.
Values may be sent and summed in bfloat16 or wider, within the bound.
A program may use at most 128 MiB of HBM per device.

v0:
```python
import jax
import jax.numpy as jnp
from jax import lax
from jax.sharding import PartitionSpec as P


def on_device(
    head_outputs, out_weight, residual, norm_gain, chosen, gates, place, w_gate, w_up, w_down
):
    tensor_count = lax.axis_size("tensor")
    replica_count = lax.axis_size("dp")
    owners = replica_count * tensor_count
    my_index = lax.axis_index("dp") * tensor_count + lax.axis_index("tensor")
    row_count = residual.shape[0]
    model_width = residual.shape[1]
    projected = lax.psum_scatter(
        jnp.dot(head_outputs, out_weight, preferred_element_type=jnp.float32).astype(jnp.bfloat16),
        "tensor",
        scatter_dimension=0,
        tiled=True,
    ).astype(jnp.float32)
    layer_state = residual.astype(jnp.float32) + projected
    scale = lax.rsqrt(jnp.mean(layer_state * layer_state, axis=1, keepdims=True) + 1.0)
    normed = (layer_state * scale * norm_gain[None, :]).astype(jnp.bfloat16)
    experts = place.shape[0]
    capacity = chosen.shape[1]
    most = 2 * capacity // owners
    pair_map = (place[None, :] == jnp.arange(experts, dtype=jnp.int32)[:, None]).astype(jnp.float32)
    chosen_pair = jnp.dot(
        pair_map, chosen.astype(jnp.float32), precision=lax.Precision.HIGHEST
    ).astype(jnp.int32)
    gates_pair = jnp.dot(pair_map, gates, precision=lax.Precision.HIGHEST)
    local_row = chosen_pair - my_index * row_count
    is_mine = (local_row >= 0) & (local_row < row_count)
    mine_float = is_mine.astype(jnp.float32)
    capacity_ids = jnp.arange(capacity, dtype=jnp.int32)
    earlier = (capacity_ids[:, None] < capacity_ids[None, :]).astype(jnp.float32)
    slot_rank = jnp.dot(mine_float, earlier, precision=lax.Precision.HIGHEST).astype(jnp.int32)
    matches = is_mine[:, :, None] & (
        slot_rank[:, :, None] == jnp.arange(most, dtype=jnp.int32)[None, None, :]
    )
    match_count = matches.astype(jnp.int32)
    send_row = jnp.sum(match_count * local_row[:, :, None], axis=1)
    send_valid = jnp.sum(match_count, axis=1) > 0
    send_gate = jnp.sum(jnp.where(matches, gates_pair[:, :, None], 0.0), axis=1)
    targets = send_row.reshape(-1)
    valid_flat = send_valid.reshape(-1)
    row_ids = jnp.arange(row_count, dtype=jnp.int32)
    selector = ((targets[:, None] == row_ids[None, :]) & valid_flat[:, None]).astype(jnp.bfloat16)
    picked = jnp.dot(selector, normed, preferred_element_type=jnp.float32).astype(jnp.bfloat16)
    picked = picked.reshape(experts, most, model_width)
    outgoing = jnp.broadcast_to(picked[:, None], (experts, 2, most, model_width)).reshape(
        owners, most, model_width
    )
    received = lax.all_to_all(outgoing, ("dp", "tensor"), split_axis=0, concat_axis=0, tiled=True)
    layout = received.shape
    flat = received.reshape(-1, layout[-1])
    contract = (((1,), (1,)), ((), ()))
    gate_part = lax.dot_general(flat, w_gate[0], contract, preferred_element_type=jnp.float32)
    up_part = lax.dot_general(flat, w_up[0], contract, preferred_element_type=jnp.float32)
    hidden = (jax.nn.silu(gate_part) * up_part).astype(jnp.bfloat16)
    result = jnp.dot(hidden, w_down[0], preferred_element_type=jnp.float32).astype(jnp.bfloat16)
    returned = lax.all_to_all(
        result.reshape(layout), ("dp", "tensor"), split_axis=0, concat_axis=0, tiled=True
    )
    halves = returned.reshape(experts, 2, most, model_width).astype(jnp.float32)
    summed = (halves[:, 0] + halves[:, 1]).reshape(experts * most, model_width)
    combine = jnp.where(
        (targets[None, :] == row_ids[:, None]) & valid_flat[None, :],
        send_gate.reshape(-1)[None, :],
        0.0,
    )
    moe = jnp.dot(combine, summed, precision=lax.Precision.HIGHEST)
    return (layer_state + moe).astype(jnp.bfloat16)


def solution(mesh):
    return jax.shard_map(
        on_device,
        mesh=mesh,
        in_specs=(
            P("dp", "tensor"),
            P("tensor", None),
            P(("dp", "tensor"), None),
            P(),
            P(),
            P(),
            P(),
            P(("dp", "tensor"), None, None),
            P(("dp", "tensor"), None, None),
            P(("dp", "tensor"), None, None),
        ),
        out_specs=P(("dp", "tensor"), None),
        check_vma=False,
    )
```

profile of v0, /device:TPU:0, one launch (start us, length us, event | category | flops | bytes accessed | tf_op | source)
XLA Modules:
  0.0 403.3 jit_solution(3481228705931696390)
XLA Ops:
  6.5 1.2 copy-done
  7.8 8.9 %convolution_convert_fusion = bf16[1024,4096]{1,0:T(8,128)(2,1)} fusion(bf16[1024,512]{1,0:T(8,128)(2,1)S(1)} %copy-done, bf16[512,4096]{1,0:T(8,128)(2,1)} %param.11), kind=kOutput, calls=%fused_computation | convolution fusion | flops 4299161600 | bytes 13631488 | tf_op jit(solution)/shard_map/dot_general | solution.py:17
  16.7 0.6 copy-done.7
  17.4 0.1 compare_and_fusion
  17.5 0.2 convolution_convert_fusion.3
  17.7 0.6 convert_reduce_fusion
  18.3 0.1 gt.19
  18.5 148.5 %reduce-scatter.2.cloned.1.call-done = bf16[128,4096]{1,0:T(8,128)(2,1)} async-done(((bf16[1024,4096]{1,0:T(8,128)(2,1)}), bf16[128,4096]{1,0:T(8,128)(2,1)}) %reduce-scatter.2.cloned.1.call-update) | async-done | bytes 1048592 | tf_op jit(solution)/shard_map/reduce_scatter | solution.py:16
  167.0 1.6 multiply_reduce_fusion
  168.7 2.0 convolution_convert_fusion.2
  170.7 0.5 broadcast_in_dim.52
  171.2 98.4 %all_to_all.10 = bf16[32,16,4096]{2,1,0:T(8,128)(2,1)S(1)} all-to-all(bf16[32,16,4096]{2,1,0:T(8,128)(2,1)S(1)} %bitcast.30), channel_id=1, replica_groups=mesh['dp'=4,'tensor'=8] {'dp','tensor'}, dimensions={0} | all-to-all | bytes 8388608 | tf_op jit(solution)/shard_map/all_to_all | solution.py:55
  269.6 2.0 copy-done.4
  271.6 3.3 fusion.3
  274.9 14.1 %convolution_convert_fusion.1 = bf16[512,4096]{1,0:T(8,128)(2,1)} fusion(bf16[1,704,4096]{2,1,0:T(8,128)(2,1)} %param.19, bf16[512,4096]{1,0:T(8,128)(2,1)} %bitcast.34, bf16[1,704,4096]{2,1,0:T(8,128)(2,1)} %param.18, f32[512,704]{0,1:T(8,128)S(1)} %fusion.3), kind=kOutput, calls=%fused_computation.1 | convolution fusion | flops 5909839872 | bytes 21364736 | tf_op jit(solution)/shard_map/dot_general | solution.py:62
  289.1 3.9 all-to-all-start.1
  293.0 0.1 fusion.30
  293.1 0.1 select_reduce_fusion
  293.3 0.1 broadcast_in_dim.48
  293.3 95.2 %all-to-all-done.1 = bf16[32,16,4096]{2,1,0:T(8,128)(2,1)} async-done(((bf16[32,16,4096]{2,1,0:T(8,128)(2,1)}), bf16[32,16,4096]{2,1,0:T(8,128)(2,1)}, u32[]{:S(2)}, u32[]{:S(2)}) %all-to-all-start.1) | async-done | bytes 4194336 | tf_op jit(solution)/shard_map/all_to_all | solution.py:63
  388.5 3.3 convert.1
  391.8 0.6 slice_add_fusion
  392.5 0.6 copy-done.3
  393.0 3.5 fusion.5
  (24 shorter events, 0.2 us)
Async XLA Ops:
  6.5 1.2 copy-start
  6.5 160.5 %reduce-scatter.2.cloned.1.call-start = ((), (), s32[]{:S(2)}) async-start(), calls=%async_computation.3 | async-start | bytes 9437184 | tf_op jit(solution)/shard_map/reduce_scatter | solution.py:16
  16.6 0.7 copy-start.7
  16.6 0.7 copy-start.8
  16.6 150.4 %copy-start.2 = (bf16[128,4096]{1,0:T(8,128)(2,1)S(1)}, bf16[128,4096]{1,0:T(8,128)(2,1)}, u32[]{:S(2)}) copy-start(bf16[128,4096]{1,0:T(8,128)(2,1)} %param.12) | copy-start | bytes 3145732
  16.6 152.0 %copy-start.5 = (f32[4096]{0:T(1024)S(1)}, f32[4096]{0:T(1024)}, u32[]{:S(2)}) copy-start(f32[4096]{0:T(1024)} %param.13) | copy-start | bytes 49156
  170.7 100.9 %slice-start = ((s8[5767168]{0:T(1024)(128)(4,1)}), s8[1572864]{0:T(1024)(128)(4,1)S(1)}, s32[]{:S(2)}) async-start(s8[5767168]{0:T(1024)(128)(4,1)} %bitcast.35), calls=%async_computation.4 | async-start | bytes 3145728
  171.2 100.4 %slice-start.1 = ((s8[5767168]{0:T(1024)(128)(4,1)}), s8[4194304]{0:T(1024)(128)(4,1)S(1)}, s32[]{:S(2)}) async-start(s8[5767168]{0:T(1024)(128)(4,1)} %bitcast.35), calls=%async_computation.5 | async-start | bytes 8388608
  269.6 2.0 copy-start.4
  289.0 3.9 copy-start.6
  289.1 99.5 %all-to-all-start.1 = ((bf16[32,16,4096]{2,1,0:T(8,128)(2,1)}), bf16[32,16,4096]{2,1,0:T(8,128)(2,1)}, u32[]{:S(2)}, u32[]{:S(2)}) async-start(bf16[32,16,4096]{2,1,0:T(8,128)(2,1)} %bitcast.32), calls=%async_computation.2 | async-start | bytes 8388608 | tf_op jit(solution)/shard_map/all_to_all | solution.py:63
  391.8 1.2 copy-start.3
  391.8 4.7 %copy-start.1 = (bf16[1024,512]{1,0:T(8,128)(2,1)S(1)}, bf16[1024,512]{1,0:T(8,128)(2,1)}, u32[]{:S(2)}) copy-start(bf16[1024,512]{1,0:T(8,128)(2,1)} %param.10) | copy-start | bytes 3145732
Sparse Core Ops, SparseCore 0:
  16.8 150.1 reduce-scatter.1
where the time goes:
time: 404 us; the launch traced here: 403 us
  waiting for transfers between devices  244 us (60%)
  blocking collectives  98.4 us (24%)
  matrix products  32.2 us (8%)
  between operations  13.5 us (3%)
  other arithmetic  6.33 us (2%)
  local copies, waits for them, and re-layouts  5.23 us (1%)
    reduce_scatter x1, waiting for transfers between devices, on_device(): lax.psum_scatter(jnp.dot(head_outputs, out_weight, preferred_element_type...  149 us
    all_to_all x1, blocking collectives, on_device(): lax.all_to_all(outgoing, ('dp', 'tensor'), split_axis=0, concat_axis=0, t...  98.4 us
    all_to_all x1, waiting for transfers between devices, on_device(): lax.all_to_all(result.reshape(layout), ('dp', 'tensor'), split_axis=0, co...  95.2 us
    dot_general x1, matrix products, on_device(): jnp.dot(hidden, w_down[0], preferred_element_type=jnp.float32)  14.1 us
    dot_general x1, matrix products, on_device(): jnp.dot(head_outputs, out_weight, preferred_element_type=jnp.float32)  8.88 us
  transfers between devices with their start and end apart: 2, of which 2 were waited for; matrix products, arithmetic and copies ran while one was open for 0% of the time, Pallas kernels for 0%

commit v1 on v0

--- a/solution.py
+++ b/solution.py
@@ -1,7 +1,332 @@
+import functools
+
 import jax
 import jax.numpy as jnp
 from jax import lax
+from jax.experimental import pallas as pl
+from jax.experimental.pallas import tpu as pltpu
 from jax.sharding import PartitionSpec as P
+
+MESH = pl.DeviceIdType.MESH
+LANES = 4
+
+
+def ring_rank(position, count):
+    upper = position // (count // 2)
+    return (1 - upper) * 2 * position + upper * (2 * (count - 1 - position) + 1)
+
+
+def project_kernel(count, x_ref, w_ref, out_ref, held, term, send_sem, recv_sem):
+    dp = lax.axis_index("dp")
+    rank = lax.axis_index("tensor")
+    odd = rank % 2
+    half = rank // 2
+    here = (1 - odd) * half + odd * (count - 1 - half)
+    right = ring_rank((here + 1) % count, count)
+    left = ring_rank((here + count - 1) % count, count)
+    rows = out_ref.shape[0]
+    width = out_ref.shape[1] // LANES
+
+    def own_term(lane, block):
+        start = pl.multiple_of(ring_rank(block, count) * rows, rows)
+        return jnp.dot(
+            x_ref[pl.ds(start, rows), :],
+            w_ref[:, lane * width : (lane + 1) * width],
+            preferred_element_type=jnp.float32,
+        )
+
+    def block_of(lane, slot):
+        if lane < LANES // 2:
+            return (here + 2 * count - 1 - slot) % count
+        return (here + 1 + slot) % count
+
+    def copy(lane, slot):
+        return pltpu.make_async_remote_copy(
+            src_ref=held.at[lane, slot],
+            dst_ref=held.at[lane, slot + 1],
+            send_sem=send_sem.at[lane, slot],
+            recv_sem=recv_sem.at[lane, slot + 1],
+            device_id=(dp, right if lane < LANES // 2 else left),
+            device_id_type=MESH,
+        )
+
+    def arrival(lane, slot):
+        return pltpu.make_async_remote_copy(
+            src_ref=held.at[lane, slot],
+            dst_ref=held.at[lane, slot],
+            send_sem=send_sem.at[lane, slot],
+            recv_sem=recv_sem.at[lane, slot],
+            device_id=(dp, right if lane < LANES // 2 else left),
+            device_id_type=MESH,
+        )
+
+    order = [lane for k in range(LANES // 2) for lane in (k, LANES // 2 + k)]
+    barrier = pltpu.get_barrier_semaphore()
+    for neighbour in (left, right):
+        pl.semaphore_signal(barrier, inc=1, device_id=(dp, neighbour), device_id_type=MESH)
+    for n, lane in enumerate(order):
+        held[lane, 0] = own_term(lane, block_of(lane, 0)).astype(held.dtype)
+        if n == 0:
+            pl.semaphore_wait(barrier, 2)
+        copy(lane, 0).start()
+
+    def step(slot, carry):
+        for lane in order:
+            term[lane] = own_term(lane, block_of(lane, slot))
+        for lane in order:
+            arrival(lane, slot).wait_recv()
+            held[lane, slot] = (held[lane, slot].astype(jnp.float32) + term[lane]).astype(held.dtype)
+            copy(lane, slot).start()
+        return carry
+
+    lax.fori_loop(1, count - 1, step, 0)
+    last = count - 1
+    for lane in order:
+        term[lane] = own_term(lane, block_of(lane, last))
+    for lane in order:
+        arrival(lane, last).wait_recv()
+        out_ref[:, lane * width : (lane + 1) * width] = (
+            held[lane, last].astype(jnp.float32) + term[lane]
+        )
+
+    def drain(slot, carry):
+        for lane in order:
+            copy(lane, slot).wait_send()
+        return carry
+
+    lax.fori_loop(0, count - 1, drain, 0)
+
+
+def project(x, w, count):
+    rows = x.shape[0] // count
+    columns = w.shape[1]
+    width = columns // LANES
+    return pl.pallas_call(
+        functools.partial(project_kernel, count),
+        out_shape=jax.ShapeDtypeStruct((rows, columns), jnp.float32),
+        in_specs=[pl.BlockSpec(memory_space=pltpu.VMEM)] * 2,
+        out_specs=pl.BlockSpec(memory_space=pltpu.VMEM),
+        scratch_shapes=[
+            pltpu.VMEM((LANES, count, rows, width), jnp.bfloat16),
+            pltpu.VMEM((LANES, rows, width), jnp.float32),
+            pltpu.SemaphoreType.DMA((LANES, count)),
+            pltpu.SemaphoreType.DMA((LANES, count)),
+        ],
+        compiler_params=pltpu.CompilerParams(
+            collective_id=0, has_side_effects=True, vmem_limit_bytes=48 * 1024 * 1024
+        ),
+    )(x, w)
+
+
+class Place:
+    def __init__(self, replicas, count):
+        self.dp = lax.axis_index("dp")
+        rank = lax.axis_index("tensor")
+        self.odd = rank % 2
+        self.per_row = count // 2
+        self.pairs = replicas * self.per_row
+        self.pair = self.dp * self.per_row + rank // 2
+        self.partner = (self.dp, rank + 1 - 2 * self.odd)
+
+    def device(self, pair):
+        return (pair // self.per_row, 2 * (pair % self.per_row) + self.odd)
+
+    def greet(self):
+        barrier = pltpu.get_barrier_semaphore()
+
+        def signal(k, carry):
+            target = self.device((self.pair + k) % self.pairs)
+            pl.semaphore_signal(barrier, inc=1, device_id=target, device_id_type=MESH)
+            return carry
+
+        lax.fori_loop(1, self.pairs, signal, 0)
+        pl.semaphore_signal(barrier, inc=1, device_id=self.partner, device_id_type=MESH)
+        pl.semaphore_wait(barrier, self.pairs)
+
+
+def loop(start, stop, body):
+    def step(k, carry):
+        body(k)
+        return carry
+
+    lax.fori_loop(start, stop, step, 0)
+
+
+def dispatch_kernel(replicas, count, x_ref, out_ref, send_sem, pass_sem, recv_sem, local_sem):
+    at = Place(replicas, count)
+    me = 2 * at.pair + at.odd
+
+    def outward(k):
+        target = (at.pair + k) % at.pairs
+        return pltpu.make_async_remote_copy(
+            src_ref=x_ref.at[target],
+            dst_ref=out_ref.at[me],
+            send_sem=send_sem.at[k],
+            recv_sem=recv_sem.at[me],
+            device_id=at.device(target),
+            device_id_type=MESH,
+        )
+
+    def across(k):
+        slot = 2 * ((at.pair + at.pairs - k) % at.pairs) + at.odd
+        return pltpu.make_async_remote_copy(
+            src_ref=out_ref.at[slot],
+            dst_ref=out_ref.at[slot],
+            send_sem=pass_sem.at[k],
+            recv_sem=recv_sem.at[slot],
+            device_id=at.partner,
+            device_id_type=MESH,
+        )
+
+    own = pltpu.make_async_remote_copy(
+        src_ref=x_ref.at[at.pair],
+        dst_ref=out_ref.at[me],
+        send_sem=pass_sem.at[0],
+        recv_sem=recv_sem.at[me],
+        device_id=at.partner,
+        device_id_type=MESH,
+    )
+    keep = pltpu.make_async_copy(x_ref.at[at.pair], out_ref.at[me], local_sem.at[0])
+    at.greet()
+    loop(1, at.pairs, lambda k: outward(k).start())
+    own.start()
+    keep.start()
+
+    def forward(k):
+        across(k).wait_recv()
+        across(k).start()
+
+    loop(1, at.pairs, forward)
+
+    def settle(k):
+        slot = 2 * ((at.pair + at.pairs - k) % at.pairs) + 1 - at.odd
+        pltpu.make_async_remote_copy(
+            src_ref=out_ref.at[slot],
+            dst_ref=out_ref.at[slot],
+            send_sem=pass_sem.at[k],
+            recv_sem=recv_sem.at[slot],
+            device_id=at.partner,
+            device_id_type=MESH,
+        ).wait_recv()
+
+    loop(0, at.pairs, settle)
+    keep.wait()
+    own.wait_send()
+
+    def drain(k):
+        outward(k).wait_send()
+        across(k).wait_send()
+
+    loop(1, at.pairs, drain)
+
+
+def dispatch(x, replicas, count):
+    pairs = x.shape[0]
+    return pl.pallas_call(
+        functools.partial(dispatch_kernel, replicas, count),
+        out_shape=jax.ShapeDtypeStruct((2 * pairs,) + x.shape[1:], x.dtype),
+        in_specs=[pl.BlockSpec(memory_space=pltpu.VMEM)],
+        out_specs=pl.BlockSpec(memory_space=pl.ANY),
+        scratch_shapes=[
+            pltpu.SemaphoreType.DMA((pairs,)),
+            pltpu.SemaphoreType.DMA((pairs,)),
+            pltpu.SemaphoreType.DMA((2 * pairs,)),
+            pltpu.SemaphoreType.DMA((1,)),
+        ],
+        compiler_params=pltpu.CompilerParams(
+            collective_id=1, has_side_effects=True, vmem_limit_bytes=48 * 1024 * 1024
+        ),
+    )(x)
+
+
+def give_back_kernel(
+    replicas, count, y_ref, out_ref, part, pass_sem, part_sem, send_sem, recv_sem, local_sem
+):
+    at = Place(replicas, count)
+
+    def across(k):
+        target = (at.pair + k) % at.pairs
+        return pltpu.make_async_remote_copy(
+            src_ref=y_ref.at[2 * target + 1 - at.odd],
+            dst_ref=part.at[target],
+            send_sem=pass_sem.at[k],
+            recv_sem=part_sem.at[target],
+            device_id=at.partner,
+            device_id_type=MESH,
+        )
+
+    def home(k):
+        target = (at.pair + k) % at.pairs
+        return pltpu.make_async_remote_copy(
+            src_ref=part.at[target],
+            dst_ref=out_ref.at[at.pair],
+            send_sem=send_sem.at[k],
+            recv_sem=recv_sem.at[at.pair],
+            device_id=at.device(target),
+            device_id_type=MESH,
+        )
+
+    def add(k):
+        across(k).wait_recv()
+        target = (at.pair + k) % at.pairs
+        part[target] = (
+            part[target].astype(jnp.float32) + y_ref[2 * target + at.odd].astype(jnp.float32)
+        ).astype(part.dtype)
+
+    at.greet()
+    loop(1, at.pairs, lambda k: across(k).start())
+    across(0).start()
+
+    def step(k):
+        add(k)
+        home(k).start()
+
+    loop(1, at.pairs, step)
+    add(0)
+    keep = pltpu.make_async_copy(part.at[at.pair], out_ref.at[at.pair], local_sem.at[0])
+    keep.start()
+
+    def settle(k):
+        source = (at.pair + at.pairs - k) % at.pairs
+        pltpu.make_async_remote_copy(
+            src_ref=part.at[source],
+            dst_ref=out_ref.at[source],
+            send_sem=send_sem.at[k],
+            recv_sem=recv_sem.at[source],
+            device_id=at.partner,
+            device_id_type=MESH,
+        ).wait_recv()
+
+    loop(1, at.pairs, settle)
+    keep.wait()
+    across(0).wait_send()
+
+    def drain(k):
+        across(k).wait_send()
+        home(k).wait_send()
+
+    loop(1, at.pairs, drain)
+
+
+def give_back(y, replicas, count):
+    pairs = y.shape[0] // 2
+    return pl.pallas_call(
+        functools.partial(give_back_kernel, replicas, count),
+        out_shape=jax.ShapeDtypeStruct((pairs,) + y.shape[1:], y.dtype),
+        in_specs=[pl.BlockSpec(memory_space=pltpu.VMEM)],
+        out_specs=pl.BlockSpec(memory_space=pl.ANY),
+        scratch_shapes=[
+            pltpu.VMEM((pairs,) + y.shape[1:], y.dtype),
+            pltpu.SemaphoreType.DMA((pairs,)),
+            pltpu.SemaphoreType.DMA((pairs,)),
+            pltpu.SemaphoreType.DMA((pairs,)),
+            pltpu.SemaphoreType.DMA((pairs,)),
+            pltpu.SemaphoreType.DMA((1,)),
+        ],
+        compiler_params=pltpu.CompilerParams(
+            collective_id=2, has_side_effects=True, vmem_limit_bytes=48 * 1024 * 1024
+        ),
+    )(y)
 
 
 def on_device(
@@ -13,12 +338,7 @@
     my_index = lax.axis_index("dp") * tensor_count + lax.axis_index("tensor")
     row_count = residual.shape[0]
     model_width = residual.shape[1]
-    projected = lax.psum_scatter(
-        jnp.dot(head_outputs, out_weight, preferred_element_type=jnp.float32).astype(jnp.bfloat16),
-        "tensor",
-        scatter_dimension=0,
-        tiled=True,
-    ).astype(jnp.float32)
+    projected = project(head_outputs, out_weight, tensor_count)
     layer_state = residual.astype(jnp.float32) + projected
     scale = lax.rsqrt(jnp.mean(layer_state * layer_state, axis=1, keepdims=True) + 1.0)
     normed = (layer_state * scale * norm_gain[None, :]).astype(jnp.bfloat16)
@@ -49,10 +369,7 @@
     selector = ((targets[:, None] == row_ids[None, :]) & valid_flat[:, None]).astype(jnp.bfloat16)
     picked = jnp.dot(selector, normed, preferred_element_type=jnp.float32).astype(jnp.bfloat16)
     picked = picked.reshape(experts, most, model_width)
-    outgoing = jnp.broadcast_to(picked[:, None], (experts, 2, most, model_width)).reshape(
-        owners, most, model_width
-    )
-    received = lax.all_to_all(outgoing, ("dp", "tensor"), split_axis=0, concat_axis=0, tiled=True)
+    received = dispatch(picked, replica_count, tensor_count)
     layout = received.shape
     flat = received.reshape(-1, layout[-1])
     contract = (((1,), (1,)), ((), ()))
@@ -60,11 +377,8 @@
     up_part = lax.dot_general(flat, w_up[0], contract, preferred_element_type=jnp.float32)
     hidden = (jax.nn.silu(gate_part) * up_part).astype(jnp.bfloat16)
     result = jnp.dot(hidden, w_down[0], preferred_element_type=jnp.float32).astype(jnp.bfloat16)
-    returned = lax.all_to_all(
-        result.reshape(layout), ("dp", "tensor"), split_axis=0, concat_axis=0, tiled=True
-    )
-    halves = returned.reshape(experts, 2, most, model_width).astype(jnp.float32)
-    summed = (halves[:, 0] + halves[:, 1]).reshape(experts * most, model_width)
+    returned = give_back(result.reshape(layout), replica_count, tensor_count)
+    summed = returned.reshape(experts * most, model_width).astype(jnp.float32)
     combine = jnp.where(
         (targets[None, :] == row_ids[:, None]) & valid_flat[None, :],
         send_gate.reshape(-1)[None, :],

time: 404 us -> 240 us (0.59)
  waiting for transfers between devices: 244 us -> 0 us
  Pallas kernels: 0 us -> 209 us
  blocking collectives: 98.4 us -> 0 us
  between operations: 13.5 us -> 0.13 us
  matrix products: 32.2 us -> 25.9 us
  other arithmetic: 6.33 us -> 1.14 us
    pallas_call x0 -> x3, Pallas kernels: none -> 209 us  [the longest x1 86.9 us: project(): pl.pallas_call(functools.partial(project_kernel, count), out_shape=jax.Sh...]
    reduce_scatter x1 -> x0, waiting for transfers between devices: 149 us -> none  [on_device(): lax.psum_scatter(jnp.dot(head_outputs, out_weight, preferred_element_type...]
    all_to_all x1 -> x0, blocking collectives: 98.4 us -> none  [on_device(): lax.all_to_all(outgoing, ('dp', 'tensor'), split_axis=0, concat_axis=0, t...]
    all_to_all x1 -> x0, waiting for transfers between devices: 95.2 us -> none  [on_device(): lax.all_to_all(result.reshape(layout), ('dp', 'tensor'), split_axis=0, co...]
    dot_general x1 -> x0, matrix products: 8.88 us -> none  [on_device(): jnp.dot(head_outputs, out_weight, preferred_element_type=jnp.float32)]
  transfers between devices with their start and end apart: 2 -> 0, of which waited for: 2 -> 0; matrix products, arithmetic and copies ran while one was open for 0% -> 0% of each run, Pallas kernels for 0% -> 0%
where the time goes in v1:
time: 240 us; the launch traced here: 239 us
  Pallas kernels  209 us (87%)
  matrix products  25.9 us (11%)
  local copies, waits for them, and re-layouts  2.53 us (1%)
    pallas_call x1, Pallas kernels, project(): pl.pallas_call(functools.partial(project_kernel, count), out_shape=jax.Sh...  86.9 us
    pallas_call x1, Pallas kernels, dispatch(): pl.pallas_call(functools.partial(dispatch_kernel, replicas, count), out_s...  62.3 us
    pallas_call x1, Pallas kernels, give_back(): pl.pallas_call(functools.partial(give_back_kernel, replicas, count), out_...  60.2 us
    dot_general x1, matrix products, on_device(): jnp.dot(hidden, w_down[0], preferred_element_type=jnp.float32)  14.5 us
    dot_general x1, matrix products, on_device(): lax.dot_general(flat, w_gate[0], contract, preferred_element_type=jnp.flo...  6.55 us

profile of v1, /device:TPU:0, one launch (start us, length us, event | category | flops | bytes accessed | tf_op | source)
XLA Modules:
  0.0 239.1 jit_solution(12072240500297386447)
XLA Ops:
  0.0 0.0 copy-start
  0.0 0.7 copy-done
  0.7 0.8 fusion.30
  1.5 0.9 compare_and_fusion
  2.4 0.2 convolution_convert_fusion.2
  2.5 0.1 select_reduce_fusion
  2.7 0.6 convert_reduce_fusion
  3.3 0.1 broadcast_in_dim.24
  3.4 0.1 gt.19
  3.5 0.1 eq.60
  3.6 1.2 copy-done.1
  4.8 86.9 %shard_map.100 = f32[128,4096]{1,0:T(8,128)S(1)} custom-call(bf16[1024,512]{1,0:T(8,128)(2,1)S(1)} %copy-done.1, bf16[512,4096]{1,0:T(8,128)(2,1)} %w_ref.1), custom_call_target="tpu_custom_call" | custom-call | tf_op jit(solution)/shard_map/pallas_call | solution.py:104
  91.8 0.0 copy-done.2
  91.8 0.0 copy-start.3
  91.8 0.0 slice-start
  91.8 0.4 multiply_reduce_fusion
  92.2 0.3 copy-done.3
  92.5 0.8 convolution_convert_fusion.1
  93.3 62.3 %shard_map.101 = bf16[32,16,4096]{2,1,0:T(8,128)(2,1)} custom-call(bf16[16,16,4096]{2,1,0:T(8,128)(2,1)S(1)} %bitcast.24), custom_call_target="tpu_custom_call" | custom-call | tf_op jit(solution)/shard_map/pallas_call | solution.py:225
  155.6 0.0 slice-done
  155.6 6.6 %fusion.3 = f32[512,704]{0,1:T(8,128)} fusion(bf16[512,4096]{1,0:T(8,128)(2,1)} %bitcast.26, bf16[1,704,4096]{2,1,0:T(8,128)(2,1)S(1)} %bitcast.30), kind=kOutput, calls=%fused_computation.4 | convolution fusion | flops 2952790016 | bytes 11403264 | tf_op jit(solution)/shard_map/dot_general | solution.py:376
  162.2 14.5 %convolution_convert_fusion = bf16[512,4096]{1,0:T(8,128)(2,1)} fusion(bf16[1,704,4096]{2,1,0:T(8,128)(2,1)} %param.19, bf16[512,4096]{1,0:T(8,128)(2,1)} %bitcast.27, bf16[1,704,4096]{2,1,0:T(8,128)(2,1)} %param.18, f32[512,704]{0,1:T(8,128)} %fusion.3), kind=kOutput, calls=%fused_computation | convolution fusion | flops 5909839872 | bytes 21364736 | tf_op jit(solution)/shard_map/dot_general | solution.py:379
  176.7 60.2 %shard_map.102 = bf16[16,16,4096]{2,1,0:T(8,128)(2,1)S(1)} custom-call(bf16[32,16,4096]{2,1,0:T(8,128)(2,1)} %bitcast.28), custom_call_target="tpu_custom_call" | custom-call | tf_op jit(solution)/shard_map/pallas_call | solution.py:313
  236.9 2.2 fusion.5
  (7 shorter events, 0.0 us)
Async XLA Ops:
  0.0 0.7 copy-start
  3.6 1.2 copy-start.1
  4.8 87.0 %copy-start.2 = (bf16[128,4096]{1,0:T(8,128)(2,1)S(1)}, bf16[128,4096]{1,0:T(8,128)(2,1)}, u32[]{:S(2)}) copy-start(bf16[128,4096]{1,0:T(8,128)(2,1)} %param.12) | copy-start | bytes 3145732
  91.8 0.7 copy-start.3
  91.8 63.8 %slice-start = ((s8[5767168]{0:T(1024)(128)(4,1)}), s8[1572864]{0:T(1024)(128)(4,1)S(1)}, s32[]{:S(2)}) async-start(s8[5767168]{0:T(1024)(128)(4,1)} %bitcast.29), calls=%async_computation | async-start | bytes 3145728
  92.5 63.1 %slice-start.1 = ((s8[5767168]{0:T(1024)(128)(4,1)}), s8[4194304]{0:T(1024)(128)(4,1)S(1)}, s32[]{:S(2)}) async-start(s8[5767168]{0:T(1024)(128)(4,1)} %bitcast.29), calls=%async_computation.1 | async-start | bytes 8388608

commit v2 on v1

--- a/solution.py
+++ b/solution.py
@@ -152,181 +152,213 @@
     lax.fori_loop(start, stop, step, 0)
 
 
-def dispatch_kernel(replicas, count, x_ref, out_ref, send_sem, pass_sem, recv_sem, local_sem):
+PIECES = 4
+
+
+def experts_kernel(
+    replicas,
+    count,
+    group,
+    x_ref,
+    gate_hbm,
+    up_hbm,
+    down_hbm,
+    out_ref,
+    gate_w,
+    up_w,
+    down_w,
+    received,
+    result,
+    part,
+    weight_sem,
+    send_sem,
+    pass_sem,
+    recv_sem,
+    cross_sem,
+    part_sem,
+    home_sem,
+    done_sem,
+    keep_sem,
+):
     at = Place(replicas, count)
-    me = 2 * at.pair + at.odd
+    most, width = x_ref.shape[1:]
+    rows = group * 2 * most
+    groups = at.pairs // group
+
+    def source(k):
+        return (at.pair + at.pairs - k) % at.pairs
 
     def outward(k):
         target = (at.pair + k) % at.pairs
         return pltpu.make_async_remote_copy(
             src_ref=x_ref.at[target],
-            dst_ref=out_ref.at[me],
+            dst_ref=received.at[k, at.odd],
             send_sem=send_sem.at[k],
-            recv_sem=recv_sem.at[me],
+            recv_sem=recv_sem.at[k, at.odd],
             device_id=at.device(target),
             device_id_type=MESH,
         )
 
+    def sideways(k, side):
+        return pltpu.make_async_remote_copy(
+            src_ref=received.at[k, side],
+            dst_ref=received.at[k, side],
+            send_sem=pass_sem.at[k],
+            recv_sem=recv_sem.at[k, side],
+            device_id=at.partner,
+            device_id_type=MESH,
+        )
+
     def across(k):
-        slot = 2 * ((at.pair + at.pairs - k) % at.pairs) + at.odd
-        return pltpu.make_async_remote_copy(
-            src_ref=out_ref.at[slot],
-            dst_ref=out_ref.at[slot],
-            send_sem=pass_sem.at[k],
-            recv_sem=recv_sem.at[slot],
+        return pltpu.make_async_remote_copy(
+            src_ref=result.at[k, 1 - at.odd],
+            dst_ref=part.at[k],
+            send_sem=cross_sem.at[k],
+            recv_sem=part_sem.at[k],
             device_id=at.partner,
             device_id_type=MESH,
         )
 
+    def home(k):
+        return pltpu.make_async_remote_copy(
+            src_ref=part.at[k],
+            dst_ref=out_ref.at[at.pair],
+            send_sem=home_sem.at[k],
+            recv_sem=done_sem.at[at.pair],
+            device_id=at.device(source(k)),
+            device_id_type=MESH,
+        )
+
+    def forward(k):
+        sideways(k, at.odd).wait_recv()
+        sideways(k, at.odd).start()
+
+    def add(k):
+        across(k).wait_recv()
+        part[k] = (
+            part[k].astype(jnp.float32) + result[k, at.odd].astype(jnp.float32)
+        ).astype(part.dtype)
+
+    def add_and_send(k):
+        add(k)
+        home(k).start()
+
+    loads = [
+        pltpu.make_async_copy(hbm.at[0], vmem, weight_sem.at[n])
+        for n, (hbm, vmem) in enumerate(((gate_hbm, gate_w), (up_hbm, up_w), (down_hbm, down_w)))
+    ]
+    for load in loads:
+        load.start()
     own = pltpu.make_async_remote_copy(
         src_ref=x_ref.at[at.pair],
-        dst_ref=out_ref.at[me],
+        dst_ref=received.at[0, at.odd],
         send_sem=pass_sem.at[0],
-        recv_sem=recv_sem.at[me],
+        recv_sem=recv_sem.at[0, at.odd],
         device_id=at.partner,
         device_id_type=MESH,
     )
-    keep = pltpu.make_async_copy(x_ref.at[at.pair], out_ref.at[me], local_sem.at[0])
     at.greet()
     loop(1, at.pairs, lambda k: outward(k).start())
     own.start()
+    received[0, at.odd] = x_ref[at.pair]
+    loop(1, group, forward)
+    for load in loads:
+        load.wait()
+    contract = (((1,), (1,)), ((), ()))
+
+    def step(g):
+        first = g * group
+
+        def forward_piece(piece):
+            @pl.when(g + 1 < groups)
+            def _():
+                start = first + group
+                cut = [start + n * group // PIECES for n in (piece, piece + 1)]
+                loop(cut[0], cut[1], forward)
+
+        loop(first, first + group, lambda k: sideways(k, 1 - at.odd).wait_recv())
+        x = received[pl.ds(first, group)].reshape(rows, width)
+        gate_part = lax.dot_general(x, gate_w[...], contract, preferred_element_type=jnp.float32)
+        forward_piece(0)
+        up_part = lax.dot_general(x, up_w[...], contract, preferred_element_type=jnp.float32)
+        hidden = (gate_part / (1.0 + jnp.exp(-gate_part)) * up_part).astype(result.dtype)
+
+        @pl.when(g > 0)
+        def _():
+            loop(jnp.maximum(first - group, 1), first, add_and_send)
+
+        forward_piece(1)
+        for piece in range(2):
+            columns = slice(piece * (width // 2), (piece + 1) * (width // 2))
+            y = jnp.dot(hidden, down_w[:, columns], preferred_element_type=jnp.float32)
+            result[pl.ds(first, group), :, :, columns] = y.astype(result.dtype).reshape(
+                group, 2, most, width // 2
+            )
+            forward_piece(2 + piece)
+        loop(first, first + group, lambda k: across(k).start())
+
+    loop(0, groups, step)
+    loop(at.pairs - group, at.pairs, add_and_send)
+    add(0)
+    keep = pltpu.make_async_copy(part.at[0], out_ref.at[at.pair], keep_sem.at[0])
     keep.start()
 
-    def forward(k):
-        across(k).wait_recv()
-        across(k).start()
-
-    loop(1, at.pairs, forward)
-
     def settle(k):
-        slot = 2 * ((at.pair + at.pairs - k) % at.pairs) + 1 - at.odd
+        pair = source(k)
         pltpu.make_async_remote_copy(
-            src_ref=out_ref.at[slot],
-            dst_ref=out_ref.at[slot],
-            send_sem=pass_sem.at[k],
-            recv_sem=recv_sem.at[slot],
+            src_ref=part.at[k],
+            dst_ref=out_ref.at[pair],
+            send_sem=home_sem.at[k],
+            recv_sem=done_sem.at[pair],
             device_id=at.partner,
             device_id_type=MESH,
         ).wait_recv()
 
-    loop(0, at.pairs, settle)
+    loop(1, at.pairs, settle)
     keep.wait()
     own.wait_send()
+    across(0).wait_send()
 
     def drain(k):
         outward(k).wait_send()
+        sideways(k, at.odd).wait_send()
         across(k).wait_send()
+        home(k).wait_send()
 
     loop(1, at.pairs, drain)
 
 
-def dispatch(x, replicas, count):
-    pairs = x.shape[0]
+def experts_layer(x, w_gate, w_up, w_down, replicas, count):
+    pairs, most, width = x.shape
+    group = min(pairs // 2, max(PIECES, 64 // most))
+    hidden_units = w_gate.shape[1]
+    weight = pltpu.VMEM((hidden_units, width), w_gate.dtype)
     return pl.pallas_call(
-        functools.partial(dispatch_kernel, replicas, count),
-        out_shape=jax.ShapeDtypeStruct((2 * pairs,) + x.shape[1:], x.dtype),
-        in_specs=[pl.BlockSpec(memory_space=pltpu.VMEM)],
+        functools.partial(experts_kernel, replicas, count, group),
+        out_shape=jax.ShapeDtypeStruct(x.shape, x.dtype),
+        in_specs=[pl.BlockSpec(memory_space=pltpu.VMEM)] + [pl.BlockSpec(memory_space=pl.ANY)] * 3,
         out_specs=pl.BlockSpec(memory_space=pl.ANY),
         scratch_shapes=[
-            pltpu.SemaphoreType.DMA((pairs,)),
-            pltpu.SemaphoreType.DMA((pairs,)),
-            pltpu.SemaphoreType.DMA((2 * pairs,)),
+            weight,
+            weight,
+            weight,
+            pltpu.VMEM((pairs, 2, most, width), x.dtype),
+            pltpu.VMEM((pairs, 2, most, width), x.dtype),
+            pltpu.VMEM((pairs, most, width), x.dtype),
+            pltpu.SemaphoreType.DMA((3,)),
+            pltpu.SemaphoreType.DMA((pairs,)),
+            pltpu.SemaphoreType.DMA((pairs,)),
+            pltpu.SemaphoreType.DMA((pairs, 2)),
+            pltpu.SemaphoreType.DMA((pairs,)),
+            pltpu.SemaphoreType.DMA((pairs,)),
+            pltpu.SemaphoreType.DMA((pairs,)),
+            pltpu.SemaphoreType.DMA((pairs,)),
             pltpu.SemaphoreType.DMA((1,)),
         ],
         compiler_params=pltpu.CompilerParams(
-            collective_id=1, has_side_effects=True, vmem_limit_bytes=48 * 1024 * 1024
+            collective_id=1, has_side_effects=True, vmem_limit_bytes=56 * 1024 * 1024
         ),
-    )(x)
-
-
-def give_back_kernel(
-    replicas, count, y_ref, out_ref, part, pass_sem, part_sem, send_sem, recv_sem, local_sem
-):
-    at = Place(replicas, count)
-
-    def across(k):
-        target = (at.pair + k) % at.pairs
-        return pltpu.make_async_remote_copy(
-            src_ref=y_ref.at[2 * target + 1 - at.odd],
-            dst_ref=part.at[target],
-            send_sem=pass_sem.at[k],
-            recv_sem=part_sem.at[target],
-            device_id=at.partner,
-            device_id_type=MESH,
-        )
-
-    def home(k):
-        target = (at.pair + k) % at.pairs
-        return pltpu.make_async_remote_copy(
-            src_ref=part.at[target],
-            dst_ref=out_ref.at[at.pair],
-            send_sem=send_sem.at[k],
-            recv_sem=recv_sem.at[at.pair],
-            device_id=at.device(target),
-            device_id_type=MESH,
-        )
-
-    def add(k):
-        across(k).wait_recv()
-        target = (at.pair + k) % at.pairs
-        part[target] = (
-            part[target].astype(jnp.float32) + y_ref[2 * target + at.odd].astype(jnp.float32)
-        ).astype(part.dtype)
-
-    at.greet()
-    loop(1, at.pairs, lambda k: across(k).start())
-    across(0).start()
-
-    def step(k):
-        add(k)
-        home(k).start()
-
-    loop(1, at.pairs, step)
-    add(0)
-    keep = pltpu.make_async_copy(part.at[at.pair], out_ref.at[at.pair], local_sem.at[0])
-    keep.start()
-
-    def settle(k):
-        source = (at.pair + at.pairs - k) % at.pairs
-        pltpu.make_async_remote_copy(
-            src_ref=part.at[source],
-            dst_ref=out_ref.at[source],
-            send_sem=send_sem.at[k],
-            recv_sem=recv_sem.at[source],
-            device_id=at.partner,
-            device_id_type=MESH,
-        ).wait_recv()
-
-    loop(1, at.pairs, settle)
-    keep.wait()
-    across(0).wait_send()
-
-    def drain(k):
-        across(k).wait_send()
-        home(k).wait_send()
-
-    loop(1, at.pairs, drain)
-
-
-def give_back(y, replicas, count):
-    pairs = y.shape[0] // 2
-    return pl.pallas_call(
-        functools.partial(give_back_kernel, replicas, count),
-        out_shape=jax.ShapeDtypeStruct((pairs,) + y.shape[1:], y.dtype),
-        in_specs=[pl.BlockSpec(memory_space=pltpu.VMEM)],
-        out_specs=pl.BlockSpec(memory_space=pl.ANY),
-        scratch_shapes=[
-            pltpu.VMEM((pairs,) + y.shape[1:], y.dtype),
-            pltpu.SemaphoreType.DMA((pairs,)),
-            pltpu.SemaphoreType.DMA((pairs,)),
-            pltpu.SemaphoreType.DMA((pairs,)),
-            pltpu.SemaphoreType.DMA((pairs,)),
-            pltpu.SemaphoreType.DMA((1,)),
-        ],
-        compiler_params=pltpu.CompilerParams(
-            collective_id=2, has_side_effects=True, vmem_limit_bytes=48 * 1024 * 1024
-        ),
-    )(y)
+    )(x, w_gate, w_up, w_down)
 
 
 def on_device(
@@ -369,15 +401,7 @@
     selector = ((targets[:, None] == row_ids[None, :]) & valid_flat[:, None]).astype(jnp.bfloat16)
     picked = jnp.dot(selector, normed, preferred_element_type=jnp.float32).astype(jnp.bfloat16)
     picked = picked.reshape(experts, most, model_width)
-    received = dispatch(picked, replica_count, tensor_count)
-    layout = received.shape
-    flat = received.reshape(-1, layout[-1])
-    contract = (((1,), (1,)), ((), ()))
-    gate_part = lax.dot_general(flat, w_gate[0], contract, preferred_element_type=jnp.float32)
-    up_part = lax.dot_general(flat, w_up[0], contract, preferred_element_type=jnp.float32)
-    hidden = (jax.nn.silu(gate_part) * up_part).astype(jnp.bfloat16)
-    result = jnp.dot(hidden, w_down[0], preferred_element_type=jnp.float32).astype(jnp.bfloat16)
-    returned = give_back(result.reshape(layout), replica_count, tensor_count)
+    returned = experts_layer(picked, w_gate, w_up, w_down, replica_count, tensor_count)
     summed = returned.reshape(experts * most, model_width).astype(jnp.float32)
     combine = jnp.where(
         (targets[None, :] == row_ids[:, None]) & valid_flat[None, :],

time: 240 us -> 219 us (0.912)
  matrix products: 25.9 us -> 7.63 us
  Pallas kernels: 209 us -> 206 us
    dot_general x2 -> x0, matrix products: 21 us -> none  [the longest x1 14.5 us: on_device(): jnp.dot(hidden, w_down[0], preferred_element_type=jnp.float32)]
    pallas_call x2 -> x1, Pallas kernels: 123 us -> 119 us  [experts_layer(): pl.pallas_call(functools.partial(experts_kernel, replicas, count, group),...]
where the time goes in v2:
time: 219 us; the launch traced here: 218 us
  Pallas kernels  206 us (94%)
  matrix products  7.63 us (3%)
  local copies, waits for them, and re-layouts  2.53 us (1%)
    pallas_call x1, Pallas kernels, experts_layer(): pl.pallas_call(functools.partial(experts_kernel, replicas, count, group),...  119 us
    pallas_call x1, Pallas kernels, project(): pl.pallas_call(functools.partial(project_kernel, count), out_shape=jax.Sh...  86.9 us

profile of v2, /device:TPU:0, one launch (start us, length us, event | category | flops | bytes accessed | tf_op | source)
XLA Modules:
  0.0 217.8 jit_solution(3436741195735199007)
XLA Ops:
  0.0 0.0 copy-start
  0.0 0.7 copy-done
  0.7 0.8 fusion.17
  1.5 0.9 compare_and_fusion
  2.4 0.2 convolution_convert_fusion.1
  2.5 0.1 select_reduce_fusion
  2.7 0.6 convert_reduce_fusion
  3.3 0.1 broadcast_in_dim.24
  3.4 0.1 gt.19
  3.5 0.1 eq.60
  3.6 0.0 copy-start.1
  3.6 1.2 copy-done.1
  4.8 0.0 copy-start.2
  4.8 86.9 %shard_map.100 = f32[128,4096]{1,0:T(8,128)S(1)} custom-call(bf16[1024,512]{1,0:T(8,128)(2,1)S(1)} %copy-done.1, bf16[512,4096]{1,0:T(8,128)(2,1)} %w_ref.1), custom_call_target="tpu_custom_call" | custom-call | tf_op jit(solution)/shard_map/pallas_call | solution.py:104
  91.8 0.0 copy-done.2
  91.8 0.0 copy-start.3
  91.8 0.4 multiply_reduce_fusion
  92.2 0.3 copy-done.3
  92.5 2.2 convolution_convert_fusion
  94.6 119.5 %shard_map.101 = bf16[16,16,4096]{2,1,0:T(8,128)(2,1)} custom-call(bf16[16,16,4096]{2,1,0:T(8,128)(2,1)} %bitcast.5, bf16[1,704,4096]{2,1,0:T(8,128)(2,1)} %gate_hbm.1, bf16[1,704,4096]{2,1,0:T(8,128)(2,1)} %up_hbm.1, bf16[1,704,4096]{2,1,0:T(8,128)(2,1)} %down_hbm.1), custom_call_target="tpu_custom_call" | custom-call | tf_op jit(solution)/shard_map/pallas_call | solution.py:336
  214.1 3.7 %fusion = bf16[128,4096]{1,0:T(8,128)(2,1)} fusion(bf16[256,4096]{1,0:T(8,128)(2,1)} %bitcast.6, f32[128,4096]{1,0:T(8,128)S(1)} %shard_map.100, bf16[128,4096]{1,0:T(8,128)(2,1)S(1)} %copy-done.2, f32[256]{0:T(256)S(1)} %broadcast_in_dim.24, s32[256]{0:T(256)S(1)} %eq.60, pred[256]{0:T(512)(128)(4,1)S(1)} %gt.19), kind=kOutput, calls=%fused_computation.2 | convolution fusion | flops 1612808192 | bytes 6293760 | tf_op jit(solution)/shard_map/dot_general | solution.py:411
  (2 shorter events, 0.0 us)
Async XLA Ops:
  0.0 0.7 copy-start
  3.6 1.2 copy-start.1
  4.8 87.0 %copy-start.2 = (bf16[128,4096]{1,0:T(8,128)(2,1)S(1)}, bf16[128,4096]{1,0:T(8,128)(2,1)}, u32[]{:S(2)}) copy-start(bf16[128,4096]{1,0:T(8,128)(2,1)} %param.12) | copy-start | bytes 3145732
  91.8 0.7 copy-start.3

commit v3 on v2

--- a/solution.py
+++ b/solution.py
@@ -123,6 +123,7 @@
         self.dp = lax.axis_index("dp")
         rank = lax.axis_index("tensor")
         self.odd = rank % 2
+        self.replicas = replicas
         self.per_row = count // 2
         self.pairs = replicas * self.per_row
         self.pair = self.dp * self.per_row + rank // 2
@@ -130,6 +131,12 @@
 
     def device(self, pair):
         return (pair // self.per_row, 2 * (pair % self.per_row) + self.odd)
+
+    def shifted(self, k, sign):
+        along, over = k // self.replicas, k % self.replicas
+        row = (self.dp + self.replicas + sign * over) % self.replicas
+        column = (self.pair % self.per_row + self.per_row + sign * along) % self.per_row
+        return row * self.per_row + column
 
     def greet(self):
         barrier = pltpu.get_barrier_semaphore()
@@ -186,10 +193,10 @@
     groups = at.pairs // group
 
     def source(k):
-        return (at.pair + at.pairs - k) % at.pairs
+        return at.shifted(k, -1)
 
     def outward(k):
-        target = (at.pair + k) % at.pairs
+        target = at.shifted(k, 1)
         return pltpu.make_async_remote_copy(
             src_ref=x_ref.at[target],
             dst_ref=received.at[k, at.odd],
@@ -294,8 +301,9 @@
             result[pl.ds(first, group), :, :, columns] = y.astype(result.dtype).reshape(
                 group, 2, most, width // 2
             )
-            forward_piece(2 + piece)
         loop(first, first + group, lambda k: across(k).start())
+        forward_piece(2)
+        forward_piece(3)
 
     loop(0, groups, step)
     loop(at.pairs - group, at.pairs, add_and_send)

time: 219 us -> 236 us (1.078)
  Pallas kernels: 206 us -> 224 us
    pallas_call x1, Pallas kernels: 119 us -> 137 us  [experts_layer(): pl.pallas_call(functools.partial(experts_kernel, replicas, count, group),...]
where the time goes in v3:
time: 236 us; the launch traced here: 235 us
  Pallas kernels  224 us (95%)
  matrix products  7.63 us (3%)
  local copies, waits for them, and re-layouts  2.53 us (1%)
    pallas_call x1, Pallas kernels, experts_layer(): pl.pallas_call(functools.partial(experts_kernel, replicas, count, group),...  137 us
    pallas_call x1, Pallas kernels, project(): pl.pallas_call(functools.partial(project_kernel, count), out_shape=jax.Sh...  86.9 us

profile of v3, /device:TPU:0, one launch (start us, length us, event | category | flops | bytes accessed | tf_op | source)
XLA Modules:
  0.0 235.4 jit_solution(17471046394670663583)
XLA Ops:
  0.0 0.0 copy-start
  0.0 0.7 copy-done
  0.7 0.8 fusion.17
  1.5 0.9 compare_and_fusion
  2.4 0.2 convolution_convert_fusion.1
  2.5 0.1 select_reduce_fusion
  2.7 0.6 convert_reduce_fusion
  3.3 0.1 broadcast_in_dim.24
  3.4 0.1 gt.19
  3.5 0.1 eq.60
  3.6 0.0 copy-start.1
  3.6 1.2 copy-done.1
  4.8 0.0 copy-start.2
  4.8 86.9 %shard_map.100 = f32[128,4096]{1,0:T(8,128)S(1)} custom-call(bf16[1024,512]{1,0:T(8,128)(2,1)S(1)} %copy-done.1, bf16[512,4096]{1,0:T(8,128)(2,1)} %w_ref.1), custom_call_target="tpu_custom_call" | custom-call | tf_op jit(solution)/shard_map/pallas_call | solution.py:104
  91.8 0.0 copy-done.2
  91.8 0.0 copy-start.3
  91.8 0.4 multiply_reduce_fusion
  92.2 0.3 copy-done.3
  92.5 2.2 convolution_convert_fusion
  94.6 137.1 %shard_map.101 = bf16[16,16,4096]{2,1,0:T(8,128)(2,1)} custom-call(bf16[16,16,4096]{2,1,0:T(8,128)(2,1)} %bitcast.5, bf16[1,704,4096]{2,1,0:T(8,128)(2,1)} %gate_hbm.1, bf16[1,704,4096]{2,1,0:T(8,128)(2,1)} %up_hbm.1, bf16[1,704,4096]{2,1,0:T(8,128)(2,1)} %down_hbm.1), custom_call_target="tpu_custom_call" | custom-call | tf_op jit(solution)/shard_map/pallas_call | solution.py:344
  231.8 3.7 %fusion = bf16[128,4096]{1,0:T(8,128)(2,1)} fusion(bf16[256,4096]{1,0:T(8,128)(2,1)} %bitcast.6, f32[128,4096]{1,0:T(8,128)S(1)} %shard_map.100, bf16[128,4096]{1,0:T(8,128)(2,1)S(1)} %copy-done.2, f32[256]{0:T(256)S(1)} %broadcast_in_dim.24, s32[256]{0:T(256)S(1)} %eq.60, pred[256]{0:T(512)(128)(4,1)S(1)} %gt.19), kind=kOutput, calls=%fused_computation.2 | convolution fusion | flops 1612808192 | bytes 6293760 | tf_op jit(solution)/shard_map/dot_general | solution.py:419
  (2 shorter events, 0.0 us)
Async XLA Ops:
  0.0 0.7 copy-start
  3.6 1.2 copy-start.1
  4.8 87.0 %copy-start.2 = (bf16[128,4096]{1,0:T(8,128)(2,1)S(1)}, bf16[128,4096]{1,0:T(8,128)(2,1)}, u32[]{:S(2)}) copy-start(bf16[128,4096]{1,0:T(8,128)(2,1)} %param.12) | copy-start | bytes 3145732
  91.8 0.7 copy-start.3
